TPU v7x, 128 devices: a whole 4x4x4 slice. The times are simulated.
128 devices in a mesh: data: 1, pp: 2 (over core), ep: 64 (over z, y, x).
Axes of the slice: x: 4, y: 4, z: 4, core: 2. Of those that a mesh axis runs over, the one named last changes fastest.
Arguments:
- expert_out: bfloat16 [2, 64, 1536, 2048], P(('data', 'pp'), 'ep')
- expert_ids: int32 [2, 192, 48, 6], P(('data', 'pp'), 'ep')
- slot_ids: int32 [2, 192, 48, 6], P(('data', 'pp'), 'ep')
- gate_vals: float32 [2, 192, 48, 6], P(('data', 'pp'), 'ep')
- residual: bfloat16 [2, 192, 48, 2048], P(('data', 'pp'), 'ep')
- norm_scale: float32 [2, 2048], P('pp')
- w_query: bfloat16 [2, 2048, 16, 128], P('pp')
- w_key: bfloat16 [2, 2048, 16, 128], P('pp')
- w_value: bfloat16 [2, 2048, 16, 128], P('pp')
- w_out: bfloat16 [2, 16, 128, 2048], P('pp')
Outputs:
- output: bfloat16 [2, 192, 48, 2048], P(('data', 'pp'), 'ep')
All inputs are finite; a program needn't handle non-finite values.
Results may differ from a plain program's by a relative error of at most 0.02.
Values are sent between devices in bfloat16 or wider.
A program may use at most 1 GiB of HBM per device.

v0:
```python
import jax
import jax.numpy as jnp
from jax import lax
from jax.sharding import PartitionSpec as P

NORM_EPS = 1e-6


def attn_block(merged, scale_vec, w_query, w_key, w_value, w_out):
    head_dim = w_query.shape[-1]
    seq_len = merged.shape[1]
    resid_f32 = merged.astype(jnp.float32)
    inv_rms = lax.rsqrt(jnp.mean(resid_f32 * resid_f32, axis=-1, keepdims=True) + NORM_EPS)
    normed_in = (resid_f32 * inv_rms * scale_vec).astype(jnp.bfloat16)
    q_heads = jnp.einsum('bld,dhe->blhe', normed_in, w_query, preferred_element_type=jnp.float32).astype(jnp.bfloat16)
    k_heads = jnp.einsum('bld,dhe->blhe', normed_in, w_key, preferred_element_type=jnp.float32).astype(jnp.bfloat16)
    v_heads = jnp.einsum('bld,dhe->blhe', normed_in, w_value, preferred_element_type=jnp.float32).astype(jnp.bfloat16)
    scores = jnp.einsum('bqhe,bkhe->bhqk', q_heads, k_heads, preferred_element_type=jnp.float32) * (head_dim ** -0.5)
    causal = jnp.arange(seq_len)[:, None] >= jnp.arange(seq_len)[None, :]
    scores = jnp.where(causal, scores, -1e30)
    exp_scores = jnp.exp(scores - jnp.max(scores, axis=-1, keepdims=True))
    row_sums = jnp.sum(exp_scores, axis=-1)
    mixed_vals = jnp.einsum('bhqk,bkhe->bqhe', exp_scores.astype(jnp.bfloat16), v_heads, preferred_element_type=jnp.float32)
    attn_out = (mixed_vals / jnp.swapaxes(row_sums, -1, -2)[..., None]).astype(jnp.bfloat16)
    proj_out = jnp.einsum('crif,ife->cre', attn_out, w_out, preferred_element_type=jnp.float32).astype(jnp.bfloat16)
    return (resid_f32 + proj_out.astype(jnp.float32)).astype(jnp.bfloat16)


def solution(mesh):
    ep_size = mesh.shape['ep']
    pp_size = mesh.shape['pp']
    next_stage = [(source, (source + 1) % pp_size) for source in range(pp_size)]
    token_spec = P(('data', 'pp'), 'ep', None, None)
    weight_spec = P('pp', None, None, None)

    def body(expert_out, expert_ids, slot_ids, gate_vals, residual, norm_scale, w_query, w_key, w_value, w_out):
        local_experts, capacity, model_width = expert_out.shape[1:]
        cap_dev = capacity // ep_size
        send_buf = expert_out[0].reshape(local_experts, ep_size, cap_dev, model_width)
        received = lax.all_to_all(send_buf, 'ep', 1, 0, tiled=True).reshape(-1, model_width)
        kept_mask = slot_ids[0] >= 0
        local_slot = slot_ids[0] - lax.axis_index('ep') * cap_dev
        row_ids = jnp.where(kept_mask, expert_ids[0] * cap_dev + local_slot, 0)
        gate_used = jnp.where(kept_mask, gate_vals[0], 0.0)
        picked_rows = jnp.take(received, row_ids, axis=0)
        merged = (residual[0].astype(jnp.float32) + jnp.sum(picked_rows * gate_used[..., None], axis=-2)).astype(jnp.bfloat16)
        arrived = lax.ppermute(merged, 'pp', next_stage)
        result = attn_block(arrived, norm_scale[0], w_query[0], w_key[0], w_value[0], w_out[0])
        return result[None]

    return jax.shard_map(body, mesh=mesh, in_specs=(token_spec, token_spec, token_spec, token_spec, token_spec, P('pp', None), weight_spec, weight_spec, weight_spec, weight_spec), out_specs=token_spec, check_vma=False)
```

profile of v0, /device:TPU:0, one launch (start us, length us, event | category | flops | bytes accessed | tf_op | source)
XLA Modules:
  0.0 148.9 jit_solution(3768013105058691013)
XLA Ops:
  0.0 0.0 copy-start.1
  0.0 0.0 copy-start.3
  0.0 0.0 copy-start.2
  0.0 11.9 %all-to-all-start = ((bf16[1,64,24,2048]{3,2,0,1:T(8,128)(2,1)}), bf16[1,64,24,2048]{3,2,0,1:T(8,128)(2,1)}, u32[]{:S(2)}, u32[]{:S(2)}) async-start(bf16[1,64,24,2048]{3,2,0,1:T(8,128)(2,1)} %bitcast.91), calls=%async_computation | async-start | bytes 12582912 | tf_op jit(solution)/shard_map/all_to_all | solution.py:40
  12.0 0.0 copy-done.1
  12.0 0.0 copy-done.3
  12.0 0.1 copy.17
  12.1 0.1 reshape.104
  12.3 0.7 copy.16
  13.0 0.0 copy-done.2
  13.0 0.7 copy.26
  13.7 88.5 %all-to-all-done = bf16[1,64,24,2048]{3,2,0,1:T(8,128)(2,1)} async-done(((bf16[1,64,24,2048]{3,2,0,1:T(8,128)(2,1)}), bf16[1,64,24,2048]{3,2,0,1:T(8,128)(2,1)}, u32[]{:S(2)}, u32[]{:S(2)}) %all-to-all-start) | async-done | bytes 6291488 | tf_op jit(solution)/shard_map/all_to_all | solution.py:40
  102.2 11.9 %gather_fusion = bf16[864,2048]{1,0:T(8,128)(2,1)S(1)} fusion(bf16[1536,2048]{1,0:T(8,128)(2,1)} %bitcast.2, s32[1024]{0:T(1024)S(1)} %pad_clamp_fusion), kind=kCustom, calls=%fused_computation | custom fusion | bytes 7081344 | tf_op jit(solution)/shard_map/jit(_take)/gather | solution.py:45
  114.1 3.5 %reshape.103 = bf16[3,48,6,2048]{3,2,1,0:T(8,128)(2,1)} reshape(bf16[864,2048]{1,0:T(8,128)(2,1)S(1)} %gather_fusion) | data formatting | bytes 7077888 | tf_op jit(solution)/shard_map/jit(_take)/gather | solution.py:45
  117.6 0.0 copy-start
  117.6 6.7 %multiply_reduce_fusion = f32[3,48,2048]{2,1,0:T(8,128)S(1)} fusion(f32[3,48,6]{2,1,0:T(8,128)} %bitcast.92, bf16[3,48,6,2048]{3,2,1,0:T(8,128)(2,1)} %reshape.103, pred[3,48,6]{2,1,0:T(8,128)(4,1)} %copy.16), kind=kLoop, calls=%fused_computation.1 | loop fusion | flops 6782976 | bytes 4722912 | tf_op jit(solution)/shard_map/reduce_sum | solution.py:46
  124.4 0.0 copy-done
  124.4 0.0 copy-start.4
  124.4 0.1 fusion.44
  124.5 0.3 collective-permute-start
  124.8 2.0 %collective-permute-done = bf16[3,48,2048]{2,1,0:T(8,128)(2,1)S(1)} collective-permute-done((bf16[3,48,2048]{2,1,0:T(8,128)(2,1)S(1)}, bf16[3,48,2048]{2,1,0:T(8,128)(2,1)S(1)}, u32[]{:S(2)}, u32[]{:S(2)}) %collective-permute-start) | collective-permute-done | bytes 589856 | tf_op jit(solution)/shard_map/ppermute | solution.py:47
  126.8 0.2 fusion.41
  127.0 0.0 copy-done.4
  127.0 5.0 %fusion.34 = bf16[3,48,16,128]{3,1,2,0:T(8,128)(2,1)S(1)} fusion(bf16[2048,16,128]{2,1,0:T(8,128)(2,1)} %bitcast.94, bf16[3,48,2048]{2,1,0:T(8,128)(2,1)S(1)} %collective-permute-done, f32[2048]{0:T(1024)S(1)} %bitcast.97, f32[3,48]{1,0:T(4,128)S(1)} %add_rsqrt_fusion), kind=kOutput, calls=%fused_computation.26 | convolution fusion | flops 1209434112 | bytes 9577024 | tf_op jit(solution)/shard_map/bld,dhe->blhe/dot_general | solution.py:15
  132.0 5.8 %fusion.59 = (f32[3,16,48]{2,1,0:T(8,128)S(1)}, f32[3,16,48,48]{2,3,1,0:T(8,128)S(1)}) fusion(bf16[3,48,16,128]{3,1,2,0:T(8,128)(2,1)S(1)} %fusion.34, bf16[2048,16,128]{2,1,0:T(8,128)(2,1)} %bitcast.95, bf16[3,48,2048]{2,1,0:T(8,128)(2,1)S(1)} %collective-permute-done, f32[2048]{0:T(1024)S(1)} %bitcast.98, f32[3,48]{1,0:T(4,128)S(1)} %add_rsqrt_fusion, ...), kind=kOutput, calls=%fused_computation.48 | convolution fusion | flops 1238075136 | bytes 10030912 | tf_op jit(solution)/shard_map/bqhe,bkhe->bhqk/dot_general | solution.py:18
  137.8 0.3 fusion.47
  138.1 5.0 %fusion.31 = bf16[3,48,16,128]{3,1,2,0:T(8,128)(2,1)S(1)} fusion(bf16[2048,16,128]{2,1,0:T(8,128)(2,1)} %bitcast.96, bf16[3,48,2048]{2,1,0:T(8,128)(2,1)S(1)} %collective-permute-done, f32[2048]{0:T(1024)S(1)} %bitcast.99, f32[3,48]{1,0:T(4,128)S(1)} %add_rsqrt_fusion), kind=kOutput, calls=%fused_computation.25 | convolution fusion | flops 1209434112 | bytes 9577024 | tf_op jit(solution)/shard_map/bld,dhe->blhe/dot_general | solution.py:17
  143.0 5.9 %fusion.26 = bf16[1,3,48,2048]{3,2,1,0:T(8,128)(2,1)} fusion(bf16[1,16,128,2048]{3,2,1,0:T(8,128)(2,1)} %param.19, bf16[3,48,2048]{2,1,0:T(8,128)(2,1)S(1)} %collective-permute-done, bf16[3,48,16,128]{3,1,2,0:T(8,128)(2,1)S(1)} %fusion.31, f32[3,16,48,48]{2,3,1,0:T(8,128)S(1)} %get-tuple-element.8, f32[3,48,16]{1,2,0:T(8,128)S(1)} %bitcast.93, ...), kind=kOutput, calls=%fused_computation.18 | convolution fusion | flops 1238556672 | bytes 10618880 | tf_op jit(solution)/shard_map/crif,ife->cre/dot_general | solution.py:25
  (6 shorter events, 0.1 us)
Async XLA Ops:
  0.0 12.0 %copy-start.1 = (s32[1,3,48,6]{2,0,3,1:T(1,128)S(1)}, s32[1,3,48,6]{2,0,3,1:T(1,128)}, u32[]{:S(2)}) copy-start(s32[1,3,48,6]{2,0,3,1:T(1,128)} %param.12) | copy-start | bytes 10372
  0.0 12.0 %copy-start.3 = (s32[1,3,48,6]{2,0,3,1:T(1,128)S(1)}, s32[1,3,48,6]{2,0,3,1:T(1,128)}, u32[]{:S(2)}) copy-start(s32[1,3,48,6]{2,0,3,1:T(1,128)} %param.11) | copy-start | bytes 10372
  0.0 13.0 %copy-start.2 = (f32[1,3,48,6]{2,0,3,1:T(1,128)S(1)}, f32[1,3,48,6]{2,0,3,1:T(1,128)}, u32[]{:S(2)}) copy-start(f32[1,3,48,6]{2,0,3,1:T(1,128)} %param.13) | copy-start | bytes 10372
  0.0 102.2 %all-to-all-start = ((bf16[1,64,24,2048]{3,2,0,1:T(8,128)(2,1)}), bf16[1,64,24,2048]{3,2,0,1:T(8,128)(2,1)}, u32[]{:S(2)}, u32[]{:S(2)}) async-start(bf16[1,64,24,2048]{3,2,0,1:T(8,128)(2,1)} %bitcast.91), calls=%async_computation | async-start | bytes 12582912 | tf_op jit(solution)/shard_map/all_to_all | solution.py:40
  117.6 6.7 %copy-start = (bf16[1,3,48,2048]{3,2,1,0:T(8,128)(2,1)S(1)}, bf16[1,3,48,2048]{3,2,1,0:T(8,128)(2,1)}, u32[]{:S(2)}) copy-start(bf16[1,3,48,2048]{3,2,1,0:T(8,128)(2,1)} %param.14) | copy-start | bytes 1769476
  124.4 2.6 %copy-start.4 = (f32[1,2048]{1,0:T(1,128)S(1)}, f32[1,2048]{1,0:T(1,128)}, u32[]{:S(2)}) copy-start(f32[1,2048]{1,0:T(1,128)} %param.15) | copy-start | bytes 24580
  124.5 2.3 %collective-permute-start = (bf16[3,48,2048]{2,1,0:T(8,128)(2,1)S(1)}, bf16[3,48,2048]{2,1,0:T(8,128)(2,1)S(1)}, u32[]{:S(2)}, u32[]{:S(2)}) collective-permute-start(bf16[3,48,2048]{2,1,0:T(8,128)(2,1)S(1)} %fusion.44), channel_id=1, source_target_pairs={{0,64},{64,0},{1,65},{65,1},{2,66},{66,2},{3,67},{67,3},{4,68},{68... | collective-permute-start | bytes 1769480 | tf_op jit(solution)/shard_map/ppermute | solution.py:47
where the time goes:
time: 151 us; the launch traced here: 149 us
  waiting for transfers between devices  90.5 us (60%)
  matrix products  21.7 us (14%)
  local copies, waits for them, and re-layouts  17.1 us (11%)
  starting transfers between devices  12.2 us (8%)
  other arithmetic  7.36 us (5%)
    all_to_all x1, waiting for transfers between devices, body(): lax.all_to_all(send_buf, 'ep', 1, 0, tiled=True).reshape(-1, model_width)  88.5 us
    gather x2, local copies, waits for them, and re-layouts, body(): picked_rows = jnp.take(received, row_ids, axis=0)  15.4 us
    all_to_all x1, starting transfers between devices, body(): lax.all_to_all(send_buf, 'ep', 1, 0, tiled=True).reshape(-1, model_width)  11.9 us
    reduce_sum x1, other arithmetic, body(): jnp.sum(picked_rows * gate_used[..., None], axis=-2)  6.7 us
    dot_general x1, matrix products, attn_block(): jnp.einsum('crif,ife->cre', attn_out, w_out, preferred_element_type=jnp.f...  5.9 us
    dot_general x1, matrix products, attn_block(): jnp.einsum('bqhe,bkhe->bhqk', q_heads, k_heads, preferred_element_type=jn...  5.82 us
    dot_general x1, matrix products, attn_block(): jnp.einsum('bld,dhe->blhe', normed_in, w_value, preferred_element_type=jn...  4.98 us
    dot_general x1, matrix products, attn_block(): jnp.einsum('bld,dhe->blhe', normed_in, w_query, preferred_element_type=jn...  4.97 us
  transfers between devices with their start and end apart: 2, of which 2 were waited for; matrix products, arithmetic and copies ran while one was open for 1% of the time, Pallas kernels for 0%

commit v1 on v0

v1 whole, which is shorter than its diff:
```python
import jax
import jax.numpy as jnp
from jax import lax
from jax.experimental import pallas as pl
from jax.experimental.pallas import tpu as pltpu
from jax.sharding import PartitionSpec as P

NORM_EPS = 1e-6
MESH = pl.DeviceIdType.MESH
ORDERS = ((2, 1, 0), (1, 0, 2), (0, 2, 1))
UNITS = ((0, 0, 512), (1, 768, 384), (2, 1408, 384), (0, 512, 256), (1, 1152, 256), (2, 1792, 256))
LENGTH = 48


def stage_kernel(o_ref, ids_ref, slots_ref, gates_ref, resid_ref, scale_ref, wq_ref, wk_ref, wv_ref, wo_ref, z_ref,
                 tq_ref, tk_ref, tv_ref, to_ref, ids, slots, gates, resid, g_buf, y_buf, x_buf, a_buf, turn,
                 ra, rc, s1, s2, s3, in1, in2, in3, sems):
    f32, bf = jnp.float32, jnp.bfloat16
    me = lax.axis_index('ep')
    core = lax.axis_index('pp')
    other = 1 - core
    m = (me // 16, (me // 4) % 4, me % 4)
    tokens, width = resid_ref.shape
    cap = o_ref.shape[3]
    n_seq, top_k = ids_ref.shape[:2]
    half = tokens // 2
    sa, xa, so, xo, sb, xb, s_two, x_two, s_one, x_one, sm, xm, sr, xr, sw = sems

    def shift(order, deltas):
        c = list(m)
        for ax, d in zip(order, deltas):
            c[ax] = (c[ax] + d) % 4
        return c

    def flat(c):
        return c[0] * 16 + c[1] * 4 + c[2]

    def dev(c, core_id):
        return {'pp': core_id, 'ep': flat(c)}

    def far(i):
        return 1 + (2 * i) % 3

    def loop(n, step):
        lax.fori_loop(0, n, lambda i, _: (step(i), 0)[1], 0)

    fetches = [pltpu.make_async_copy(w, t, sw.at[i]) for i, (w, t) in enumerate(((wq_ref, tq_ref), (wk_ref, tk_ref), (wv_ref, tv_ref), (wo_ref, to_ref)))]
    for fetch in fetches:
        fetch.start()

    barrier = pltpu.get_barrier_semaphore()

    def greet(i):
        for ax in range(3):
            for cid in (core, other):
                pl.semaphore_signal(barrier, inc=1, device_id=dev(shift((ax,), (i + 1,)), cid), device_id_type=MESH)

    loop(3, greet)
    pl.semaphore_signal(barrier, inc=1, device_id=dev(m, other), device_id_type=MESH)
    pl.semaphore_wait(barrier, 19)

    def osrc(u, a, b):
        col, first, wide = UNITS[u]
        order = ORDERS[col]
        idx = [slice(None)] * 3
        idx[order[0]] = a
        idx[order[1]] = b
        return o_ref.at[idx[0], idx[1], idx[2], :, pl.ds(first, wide)]

    def remote(src, dst, send, recv, c, core_id):
        return pltpu.make_async_remote_copy(src_ref=src, dst_ref=dst, send_sem=send, recv_sem=recv, device_id=dev(c, core_id), device_id_type=MESH)

    def cp_a(u, da, db):
        order = ORDERS[UNITS[u][0]]
        c = shift(order, (da, db, 0))
        return remote(osrc(u, c[order[0]], c[order[1]]), ra[u].at[da - 1, db - 1], sa.at[u, da - 1, db], xa.at[u, da - 1, db],
                      shift(order, (da, 0, 0)), other)

    def cp_a0(u, da):
        order = ORDERS[UNITS[u][0]]
        c = shift(order, (da, 0, 0))
        return remote(osrc(u, c[order[0]], c[order[1]]), rc[u].at[:, da * 4], sa.at[u, da - 1, 0], xa.at[u, da - 1, 0], c, other)

    def cp_own(u):
        order = ORDERS[UNITS[u][0]]
        return remote(osrc(u, m[order[0]], m[order[1]]), rc[u].at[:, 0], so.at[u], xo.at[u], m, other)

    def cp_b(u, da, db):
        return remote(ra[u].at[da - 1, db - 1], rc[u].at[:, da * 4 + db], sb.at[u, da, db - 1], xb.at[u, da, db - 1],
                      shift(ORDERS[UNITS[u][0]], (0, db, 0)), core)

    def cp_b0(u, db):
        order = ORDERS[UNITS[u][0]]
        c = shift(order, (0, db, 0))
        return remote(osrc(u, c[order[0]], c[order[1]]), rc[u].at[:, db], sb.at[u, 0, db - 1], xb.at[u, 0, db - 1], c, other)

    def line(u, d):
        return shift(ORDERS[UNITS[u][0]], (0, 0, d))

    def cp_two(u, way):
        return remote(s2[u].at[pl.ds(way * half, half)], in2[u].at[way], s_two.at[u, way], x_two.at[u, way], line(u, (1, 3)[way]), core)

    def cp_one(u, way):
        return remote((s1, s3)[way][u], (in1, in3)[way][u], s_one.at[u, way], x_one.at[u, way], line(u, (1, 3)[way]), core)

    def cp_m(ax, d, k):
        src, dst = ((ids_ref, ids), (slots_ref, slots), (gates_ref, gates))[k]
        at = 0 if ax is None else 3 * ax + (4 - d)
        return remote(src, dst.at[at], sm.at[at, k], xm.at[at, k], m if ax is None else shift((ax,), (d,)), other)

    cp_h = remote(resid_ref, resid, sr, xr, m, other)

    def each_m(f):
        for k in range(3):
            f(cp_m(None, 0, k))
            for ax in range(3):
                loop(3, lambda i, ax=ax, k=k: f(cp_m(ax, i + 1, k)))

    def turn_heads(buf, n_blocks, first):
        def step(i):
            for k in range(4):
                buf[first + i * 4 + k] = jnp.swapaxes(buf[first + i * 4 + k], 0, 1)
        loop(n_blocks // 4, step)

    def choose():
        turn[...] = jnp.zeros_like(turn)

        def spread(values, dc):
            for seq in range(n_seq):
                for j in range(top_k):
                    turn[pl.ds((dc * n_seq + seq) * top_k + j, 1), 0:LENGTH] = values[seq, j].astype(f32)

        lane = lax.broadcasted_iota(jnp.int32, (LENGTH, 16 * cap), 1)
        for col in range(3):
            order = ORDERS[col]
            for dc in range(4):
                at = 3 * order[2] + dc if dc else 0
                e, slot = ids[at], slots[at]
                ec = (e >> 4, (e >> 2) & 3, e & 3)
                place = (((m[order[0]] - ec[order[0]]) & 3) * 4 + ((m[order[1]] - ec[order[1]]) & 3)) * cap + slot - flat(shift(order, (0, 0, dc))) * cap
                spread(jnp.where((slot >= 0) & (ec[order[2]] == m[order[2]]), place, -1), dc)
            pos_t = turn[...].T.astype(jnp.int32)
            for dc in range(4):
                spread(gates[3 * order[2] + dc if dc else 0], dc)
            gate_t = turn[...].T
            for dc in range(4):
                for seq in range(n_seq):
                    g = jnp.zeros((LENGTH, 16 * cap), f32)
                    for j in range(top_k):
                        at = (dc * n_seq + seq) * top_k + j
                        g = jnp.where(pos_t[0:LENGTH, at:at + 1] == lane, gate_t[0:LENGTH, at:at + 1], g)
                    for part in range(3):
                        top = g.astype(bf)
                        g_buf[col, dc, pl.ds(part * tokens + seq * LENGTH, LENGTH), :] = top
                        g = g - top.astype(f32)

    def partial(u, dc):
        col, _, wide = UNITS[u]
        rows = rc[u][line(u, dc)[ORDERS[col][2]]].reshape(16 * cap, wide)
        acc = jnp.dot(g_buf[col, dc], rows, preferred_element_type=f32)
        return (acc[:tokens] + acc[tokens:2 * tokens]) + acc[2 * tokens:]

    def send_first(us):
        loop(9, lambda i: [cp_a(u, far(i % 3), far(i // 3)).start() for u in us])
        loop(3, lambda i: [cp_a0(u, far(i)).start() for u in us])
        for u in us:
            cp_own(u).start()
        loop(3, lambda i: [cp_b0(u, far(i)).start() for u in us])

    def pass_on(us):
        def step(i):
            for u in us:
                cp_a(u, far(i % 3), far(i // 3)).wait_recv()
                cp_b(u, far(i % 3), far(i // 3)).start()
        loop(9, step)

    def rows_landed(us):
        for u in us:
            cp_own(u).wait_recv()
        loop(3, lambda i: [cp_a0(u, i + 1).wait_recv() for u in us])
        loop(3, lambda i: [cp_b0(u, i + 1).wait_recv() for u in us])
        loop(9, lambda i: [cp_b(u, far(i // 3), far(i % 3)).wait_recv() for u in us])

    def ring_start(us):
        for u in us:
            s2[u][...] = partial(u, 2)
        for u in us:
            s1[u][...] = partial(u, 1)
            for way in range(2):
                cp_two(u, way).start()
        for u in us:
            s3[u][...] = partial(u, 3)

    def ring_next(us):
        for u in us:
            cp_two(u, 0).wait_recv()
            cp_two(u, 1).wait_recv()
            s1[u][0:half] = s1[u][0:half] + in2[u][0]
            s3[u][half:] = s3[u][half:] + in2[u][1]
        for u in us:
            for way in range(2):
                cp_one(u, way).start()

    def own_sums(us):
        for u in us:
            _, first, wide = UNITS[u]
            own = partial(u, 0)
            cp_one(u, 0).wait_recv()
            cp_one(u, 1).wait_recv()
            y_buf[:, pl.ds(first, wide)] = (resid[:, pl.ds(first, wide)].astype(f32) + ((own + in1[u][...]) + in3[u][...])).astype(bf)

    early, late = (0, 1, 2), (3, 4, 5)
    send_first(early)
    each_m(lambda c: c.start())
    cp_h.start()
    fetches[0].wait()
    turn_heads(tq_ref, 128, 0)
    pass_on(early)
    send_first(late)
    each_m(lambda c: c.wait_recv())
    choose()
    fetches[1].wait()
    turn_heads(tk_ref, 128, 0)
    fetches[2].wait()
    turn_heads(tv_ref, 128, 0)
    rows_landed(early)
    ring_start(early)
    pass_on(late)
    ring_next(early)
    cp_h.wait_recv()
    rows_landed(late)
    ring_start(late)
    own_sums(early)
    ring_next(late)
    own_sums(late)
    fetches[3].wait()

    r = y_buf[...].astype(f32)
    x_buf[...] = (r * lax.rsqrt(jnp.mean(r * r, axis=-1, keepdims=True) + NORM_EPS) * scale_ref[...]).astype(bf)

    t_row = lax.broadcasted_iota(jnp.int32, (tokens, tokens), 0)
    t_col = lax.broadcasted_iota(jnp.int32, (tokens, tokens), 1)
    keep = (t_row >= t_col) & (t_row // LENGTH == t_col // LENGTH)
    for n in range(8):
        x = x_buf[...]
        heads = [jnp.concatenate([t[:, 2 * n].reshape(width, 128), t[:, 2 * n + 1].reshape(width, 128)], axis=1) for t in (tq_ref, tk_ref, tv_ref)]
        q, k, v = [jnp.dot(x, w, preferred_element_type=f32).astype(bf) for w in heads]
        for h in range(2):
            lanes = slice(h * 128, h * 128 + 128)
            s = lax.dot_general(q[:, lanes], k[:, lanes], (((1,), (1,)), ((), ())), preferred_element_type=f32) * 128 ** -0.5
            s = jnp.where(keep, s, -1e30)
            e = jnp.exp(s - jnp.max(s, axis=-1, keepdims=True))
            mixed = jnp.dot(e.astype(bf), v[:, lanes], preferred_element_type=f32)
            a_buf[:, pl.ds((2 * n + h) * 128, 128)] = (mixed / jnp.sum(e, axis=-1, keepdims=True)).astype(bf)

    for n in range(width // 512):
        cols = pl.ds(n * 512, 512)
        proj = jnp.dot(a_buf[...], to_ref[:, cols], preferred_element_type=f32).astype(bf)
        z_ref[:, cols] = (y_buf[:, cols].astype(f32) + proj.astype(f32)).astype(bf)

    cp_h.wait_send()
    each_m(lambda c: c.wait_send())
    for u in range(6):
        cp_own(u).wait_send()
        for way in range(2):
            cp_two(u, way).wait_send()
            cp_one(u, way).wait_send()
    every = range(6)
    loop(9, lambda i: [cp_a(u, 1 + i // 3, 1 + i % 3).wait_send() for u in every])
    loop(9, lambda i: [cp_b(u, 1 + i // 3, 1 + i % 3).wait_send() for u in every])
    loop(3, lambda i: [cp_a0(u, 1 + i).wait_send() for u in every])
    loop(3, lambda i: [cp_b0(u, 1 + i).wait_send() for u in every])


def run_stage(o, ids, slots, gates, resid, scale, wq, wk, wv, wo):
    bf, f32 = jnp.bfloat16, jnp.float32
    cap, width = o.shape[3:]
    tokens = resid.shape[0]
    dma, buf = pltpu.SemaphoreType.DMA, pltpu.VMEM
    hbm, vmem = pl.BlockSpec(memory_space=pl.ANY), pl.BlockSpec(memory_space=pltpu.VMEM)
    sums = [buf((tokens, w), f32) for _, _, w in UNITS]
    pairs = [buf((2, tokens // 2, w), f32) for _, _, w in UNITS]
    sems = [dma((6, 3, 4)), dma((6, 3, 4)), dma((6,)), dma((6,)), dma((6, 4, 3)), dma((6, 4, 3)), dma((6, 2)), dma((6, 2)), dma((6, 2)), dma((6, 2)),
            dma((10, 3)), dma((10, 3)), dma(()), dma(()), dma((4,))]
    return pl.pallas_call(
        stage_kernel,
        out_shape=jax.ShapeDtypeStruct((tokens, width), bf),
        in_specs=[hbm] * 5 + [vmem] + [hbm] * 4,
        out_specs=vmem,
        scratch_shapes=[buf(wq.shape, bf)] * 3 + [buf(wo.shape, bf)]
        + [buf((10,) + ids.shape, ids.dtype), buf((10,) + slots.shape, slots.dtype), buf((10,) + gates.shape, gates.dtype), buf(resid.shape, bf)]
        + [buf((3, 4, 3 * tokens, 16 * cap), bf)] + [buf((tokens, width), bf)] * 3 + [buf((128, 128), f32)]
        + [[buf((3, 3, 4, cap, w), bf) for _, _, w in UNITS], [buf((4, 16, cap, w), bf) for _, _, w in UNITS]]
        + [sums, sums, sums, sums, pairs, sums] + [sems],
        compiler_params=pltpu.CompilerParams(collective_id=0, has_side_effects=True, vmem_limit_bytes=63 * 2**20),
    )(o, ids, slots, gates, resid, scale, wq, wk, wv, wo)


def solution(mesh):
    token_spec = P(('data', 'pp'), 'ep', None, None)
    weight_spec = P('pp', None, None, None)

    def body(expert_out, expert_ids, slot_ids, gate_vals, residual, norm_scale, w_query, w_key, w_value, w_out):
        width = expert_out.shape[-1]
        cap = expert_out.shape[2] // 64
        seqs, length, top_k = expert_ids.shape[1:]
        ids, slots, gates = [jnp.transpose(a, (1, 3, 0, 2)) for a in (expert_ids, slot_ids, gate_vals)]
        result = run_stage(expert_out[0, 0].reshape(4, 4, 4, cap, width), ids, slots, gates, residual[0].reshape(-1, width),
                           norm_scale, *[w[0].reshape(width // 16, 16, 16, 128) for w in (w_query, w_key, w_value)], w_out[0].reshape(width, width))
        return result.reshape(residual.shape)

    return jax.shard_map(body, mesh=mesh, in_specs=(token_spec, token_spec, token_spec, token_spec, token_spec, P('pp', None), weight_spec, weight_spec, weight_spec, weight_spec), out_specs=token_spec, check_vma=False)
```

time: 151 us -> 89.6 us (0.59); the launches traced: 149 us -> 89.4 us
  waiting for transfers between devices: 90.5 us -> 0 us
  Pallas kernels: 0 us -> 87.5 us
  matrix products: 21.7 us -> 0 us
  local copies, waits for them, and re-layouts: 17.1 us -> 1.93 us
  starting transfers between devices: 12.2 us -> 0 us
  other arithmetic: 7.36 us -> 0 us
    all_to_all x1 -> x0, waiting for transfers between devices: 88.5 us -> none  [body(): lax.all_to_all(send_buf, 'ep', 1, 0, tiled=True).reshape(-1, model_width)]
    pallas_call x0 -> x1, Pallas kernels: none -> 87.5 us  [run_stage(): pl.pallas_call(stage_kernel, out_shape=jax.ShapeDtypeStruct((tokens, widt...]
    dot_general x4 -> x0, matrix products: 21.7 us -> none  [the longest x1 5.9 us: attn_block(): jnp.einsum('crif,ife->cre', attn_out, w_out, preferred_element_type=jnp.f...]
    gather x2 -> x0, local copies, waits for them, and re-layouts: 15.4 us -> none  [body(): picked_rows = jnp.take(received, row_ids, axis=0)]
    all_to_all x1 -> x0, starting transfers between devices: 11.9 us -> none  [body(): lax.all_to_all(send_buf, 'ep', 1, 0, tiled=True).reshape(-1, model_width)]
    reduce_sum x3 -> x0, other arithmetic: 7.16 us -> none  [the longest x1 6.7 us: body(): jnp.sum(picked_rows * gate_used[..., None], axis=-2)]
    ppermute x1 -> x0, waiting for transfers between devices: 1.97 us -> none  [body(): arrived = lax.ppermute(merged, 'pp', next_stage)]
    unnamed x10 -> x1, local copies, waits for them, and re-layouts: 0.02 us -> 1.93 us
  transfers between devices with their start and end apart: 2 -> 0, of which waited for: 2 -> 0; matrix products, arithmetic and copies ran while one was open for 1% -> 0% of each run, Pallas kernels for 0% -> 0%
where the time goes in v1:
time: 89.6 us; the launch traced here: 89.4 us
  Pallas kernels  87.5 us (98%)
  local copies, waits for them, and re-layouts  1.93 us (2%)
    pallas_call x1, Pallas kernels, run_stage(): pl.pallas_call(stage_kernel, out_shape=jax.ShapeDtypeStruct((tokens, widt...  87.5 us
    unnamed x1, local copies, waits for them, and re-layouts  1.93 us

profile of v1, /device:TPU:0, one launch (start us, length us, event | category | flops | bytes accessed | tf_op | source)
XLA Modules:
  0.0 89.4 jit_solution(12100604481338603720)
XLA Ops:
  0.0 87.5 %shard_map.100 = bf16[144,2048]{1,0:T(8,128)(2,1)} custom-call(bf16[4,4,4,24,2048]{4,3,2,1,0:T(8,128)(2,1)} %bitcast.14, s32[3,6,1,48]{3,2,1,0:T(1,128)} %bitcast.17, s32[3,6,1,48]{3,2,1,0:T(1,128)} %bitcast.18, f32[3,6,1,48]{3,2,1,0:T(1,128)} %bitcast.19, bf16[144,2048]{1,0:T(8,128)(2,1)} %bitcast.16, f32[1,2048]{1,0:T(1,128)} %scale_ref.1, ...), custom_call_target="tpu_custom_call" | custom-call | tf_op jit(solution)/shard_map/pallas_call | solution.py:285
  87.5 1.9 %copy.12 = bf16[1,3,48,2048]{3,2,1,0:T(8,128)(2,1)} copy(bf16[1,3,48,2048]{3,2,1,0:T(8,128)(2,1)} %bitcast.15) | data formatting | bytes 1179648

commit v2 on v1

--- a/solution.py
+++ b/solution.py
@@ -13,7 +13,7 @@
 
 
 def stage_kernel(o_ref, ids_ref, slots_ref, gates_ref, resid_ref, scale_ref, wq_ref, wk_ref, wv_ref, wo_ref, z_ref,
-                 tq_ref, tk_ref, tv_ref, to_ref, ids, slots, gates, resid, g_buf, y_buf, x_buf, a_buf, turn,
+                 tq_ref, tk_ref, tv_ref, to_ref, scale, ids, slots, gates, resid, own_buf, g_buf, y_buf, x_buf, a_buf, turn,
                  ra, rc, s1, s2, s3, in1, in2, in3, sems):
     f32, bf = jnp.float32, jnp.bfloat16
     me = lax.axis_index('ep')
@@ -44,7 +44,7 @@
     def loop(n, step):
         lax.fori_loop(0, n, lambda i, _: (step(i), 0)[1], 0)
 
-    fetches = [pltpu.make_async_copy(w, t, sw.at[i]) for i, (w, t) in enumerate(((wq_ref, tq_ref), (wk_ref, tk_ref), (wv_ref, tv_ref), (wo_ref, to_ref)))]
+    fetches = [pltpu.make_async_copy(w, t, sw.at[i]) for i, (w, t) in enumerate(((wq_ref, tq_ref), (wk_ref, tk_ref), (wv_ref, tv_ref), (wo_ref, to_ref), (scale_ref, scale)))]
     for fetch in fetches:
         fetch.start()
 
@@ -182,14 +182,22 @@
         loop(9, lambda i: [cp_b(u, far(i // 3), far(i % 3)).wait_recv() for u in us])
 
     def ring_start(us):
-        for u in us:
-            s2[u][...] = partial(u, 2)
-        for u in us:
-            s1[u][...] = partial(u, 1)
+        def send(u):
             for way in range(2):
                 cp_two(u, way).start()
+        for k, u in enumerate(us):
+            s2[u][...] = partial(u, 2)
+            if k:
+                send(us[k - 1])
+        for k, u in enumerate(us):
+            s1[u][...] = partial(u, 1)
+            if k == 0:
+                send(us[-1])
         for u in us:
             s3[u][...] = partial(u, 3)
+        for u in us:
+            cols = pl.ds(UNITS[u][1], UNITS[u][2])
+            own_buf[:, cols] = resid[:, cols].astype(f32) + partial(u, 0)
 
     def ring_next(us):
         for u in us:
@@ -204,10 +212,9 @@
     def own_sums(us):
         for u in us:
             _, first, wide = UNITS[u]
-            own = partial(u, 0)
             cp_one(u, 0).wait_recv()
             cp_one(u, 1).wait_recv()
-            y_buf[:, pl.ds(first, wide)] = (resid[:, pl.ds(first, wide)].astype(f32) + ((own + in1[u][...]) + in3[u][...])).astype(bf)
+            y_buf[:, pl.ds(first, wide)] = ((own_buf[:, pl.ds(first, wide)] + in1[u][...]) + in3[u][...]).astype(bf)
 
     early, late = (0, 1, 2), (3, 4, 5)
     send_first(early)
@@ -223,28 +230,31 @@
     turn_heads(tk_ref, 128, 0)
     fetches[2].wait()
     turn_heads(tv_ref, 128, 0)
+    cp_h.wait_recv()
     rows_landed(early)
     ring_start(early)
     pass_on(late)
     ring_next(early)
-    cp_h.wait_recv()
     rows_landed(late)
     ring_start(late)
     own_sums(early)
     ring_next(late)
     own_sums(late)
     fetches[3].wait()
+    fetches[4].wait()
 
     r = y_buf[...].astype(f32)
-    x_buf[...] = (r * lax.rsqrt(jnp.mean(r * r, axis=-1, keepdims=True) + NORM_EPS) * scale_ref[...]).astype(bf)
+    x_buf[...] = (r * lax.rsqrt(jnp.mean(r * r, axis=-1, keepdims=True) + NORM_EPS) * scale[...]).astype(bf)
 
     t_row = lax.broadcasted_iota(jnp.int32, (tokens, tokens), 0)
     t_col = lax.broadcasted_iota(jnp.int32, (tokens, tokens), 1)
     keep = (t_row >= t_col) & (t_row // LENGTH == t_col // LENGTH)
-    for n in range(8):
+    def project(n):
         x = x_buf[...]
         heads = [jnp.concatenate([t[:, 2 * n].reshape(width, 128), t[:, 2 * n + 1].reshape(width, 128)], axis=1) for t in (tq_ref, tk_ref, tv_ref)]
-        q, k, v = [jnp.dot(x, w, preferred_element_type=f32).astype(bf) for w in heads]
+        return [jnp.dot(x, w, preferred_element_type=f32).astype(bf) for w in heads]
+
+    def mix(n, q, k, v):
         for h in range(2):
             lanes = slice(h * 128, h * 128 + 128)
             s = lax.dot_general(q[:, lanes], k[:, lanes], (((1,), (1,)), ((), ())), preferred_element_type=f32) * 128 ** -0.5
@@ -252,6 +262,12 @@
             e = jnp.exp(s - jnp.max(s, axis=-1, keepdims=True))
             mixed = jnp.dot(e.astype(bf), v[:, lanes], preferred_element_type=f32)
             a_buf[:, pl.ds((2 * n + h) * 128, 128)] = (mixed / jnp.sum(e, axis=-1, keepdims=True)).astype(bf)
+
+    held = project(0)
+    for n in range(8):
+        ahead = project(n + 1) if n < 7 else None
+        mix(n, *held)
+        held = ahead
 
     for n in range(width // 512):
         cols = pl.ds(n * 512, 512)
@@ -281,14 +297,14 @@
     sums = [buf((tokens, w), f32) for _, _, w in UNITS]
     pairs = [buf((2, tokens // 2, w), f32) for _, _, w in UNITS]
     sems = [dma((6, 3, 4)), dma((6, 3, 4)), dma((6,)), dma((6,)), dma((6, 4, 3)), dma((6, 4, 3)), dma((6, 2)), dma((6, 2)), dma((6, 2)), dma((6, 2)),
-            dma((10, 3)), dma((10, 3)), dma(()), dma(()), dma((4,))]
+            dma((10, 3)), dma((10, 3)), dma(()), dma(()), dma((5,))]
     return pl.pallas_call(
         stage_kernel,
-        out_shape=jax.ShapeDtypeStruct((tokens, width), bf),
-        in_specs=[hbm] * 5 + [vmem] + [hbm] * 4,
+        out_shape=pltpu.VMEM((tokens, width), bf),
+        in_specs=[hbm] * 10,
         out_specs=vmem,
-        scratch_shapes=[buf(wq.shape, bf)] * 3 + [buf(wo.shape, bf)]
-        + [buf((10,) + ids.shape, ids.dtype), buf((10,) + slots.shape, slots.dtype), buf((10,) + gates.shape, gates.dtype), buf(resid.shape, bf)]
+        scratch_shapes=[buf(wq.shape, bf)] * 3 + [buf(wo.shape, bf), buf(scale.shape, f32)]
+        + [buf((10,) + ids.shape, ids.dtype), buf((10,) + slots.shape, slots.dtype), buf((10,) + gates.shape, gates.dtype), buf(resid.shape, bf), buf(resid.shape, f32)]
         + [buf((3, 4, 3 * tokens, 16 * cap), bf)] + [buf((tokens, width), bf)] * 3 + [buf((128, 128), f32)]
         + [[buf((3, 3, 4, cap, w), bf) for _, _, w in UNITS], [buf((4, 16, cap, w), bf) for _, _, w in UNITS]]
         + [sums, sums, sums, sums, pairs, sums] + [sems],

time: 89.6 us -> 83.8 us (0.935)
  Pallas kernels: 87.5 us -> 82.9 us
  local copies, waits for them, and re-layouts: 1.93 us -> 0.82 us
    pallas_call x1, Pallas kernels: 87.5 us -> 82.9 us  [run_stage(): pl.pallas_call(stage_kernel, out_shape=pltpu.VMEM((tokens, width), bf), i...]
    unnamed x1, local copies, waits for them, and re-layouts: 1.93 us -> 0.82 us
where the time goes in v2:
time: 83.8 us; the launch traced here: 83.7 us
  Pallas kernels  82.9 us (99%)
    pallas_call x1, Pallas kernels, run_stage(): pl.pallas_call(stage_kernel, out_shape=pltpu.VMEM((tokens, width), bf), i...  82.9 us

profile of v2, /device:TPU:0, one launch (start us, length us, event | category | flops | bytes accessed | tf_op | source)
XLA Modules:
  0.0 83.7 jit_solution(6901670012011233436)
XLA Ops:
  0.0 82.9 %shard_map.100 = bf16[144,2048]{1,0:T(8,128)(2,1)S(1)} custom-call(bf16[4,4,4,24,2048]{4,3,2,1,0:T(8,128)(2,1)} %bitcast.15, s32[3,6,1,48]{3,2,1,0:T(1,128)} %bitcast.17, s32[3,6,1,48]{3,2,1,0:T(1,128)} %bitcast.18, f32[3,6,1,48]{3,2,1,0:T(1,128)} %bitcast.19, bf16[144,2048]{1,0:T(8,128)(2,1)} %bitcast.16, f32[1,2048]{1,0:T(1,128)} %scale_ref.1, ...), custom_call_target="tpu_custom_call" | custom-call | tf_op jit(solution)/shard_map/pallas_call | solution.py:301
  82.9 0.8 copy.12

commit v3 on v2

--- a/solution.py
+++ b/solution.py
@@ -216,6 +216,22 @@
             cp_one(u, 1).wait_recv()
             y_buf[:, pl.ds(first, wide)] = ((own_buf[:, pl.ds(first, wide)] + in1[u][...]) + in3[u][...]).astype(bf)
 
+    def first_left(us):
+        loop(9, lambda i: [cp_a(u, 1 + i // 3, 1 + i % 3).wait_send() for u in us])
+        loop(3, lambda i: [cp_a0(u, 1 + i).wait_send() for u in us])
+        loop(3, lambda i: [cp_b0(u, 1 + i).wait_send() for u in us])
+        for u in us:
+            cp_own(u).wait_send()
+
+    def second_left(us):
+        loop(9, lambda i: [cp_b(u, 1 + i // 3, 1 + i % 3).wait_send() for u in us])
+
+    def ring_left(us):
+        for u in us:
+            for way in range(2):
+                cp_two(u, way).wait_send()
+                cp_one(u, way).wait_send()
+
     early, late = (0, 1, 2), (3, 4, 5)
     send_first(early)
     each_m(lambda c: c.start())
@@ -235,10 +251,16 @@
     ring_start(early)
     pass_on(late)
     ring_next(early)
+    cp_h.wait_send()
+    each_m(lambda c: c.wait_send())
+    first_left(early + late)
+    second_left(early)
     rows_landed(late)
     ring_start(late)
     own_sums(early)
     ring_next(late)
+    second_left(late)
+    ring_left(early)
     own_sums(late)
     fetches[3].wait()
     fetches[4].wait()
@@ -254,38 +276,39 @@
         heads = [jnp.concatenate([t[:, 2 * n].reshape(width, 128), t[:, 2 * n + 1].reshape(width, 128)], axis=1) for t in (tq_ref, tk_ref, tv_ref)]
         return [jnp.dot(x, w, preferred_element_type=f32).astype(bf) for w in heads]
 
-    def mix(n, q, k, v):
+    def weigh(q, k):
+        out = []
         for h in range(2):
             lanes = slice(h * 128, h * 128 + 128)
             s = lax.dot_general(q[:, lanes], k[:, lanes], (((1,), (1,)), ((), ())), preferred_element_type=f32) * 128 ** -0.5
             s = jnp.where(keep, s, -1e30)
             e = jnp.exp(s - jnp.max(s, axis=-1, keepdims=True))
-            mixed = jnp.dot(e.astype(bf), v[:, lanes], preferred_element_type=f32)
-            a_buf[:, pl.ds((2 * n + h) * 128, 128)] = (mixed / jnp.sum(e, axis=-1, keepdims=True)).astype(bf)
-
-    held = project(0)
+            out.append((e.astype(bf), jnp.sum(e, axis=-1, keepdims=True)))
+        return out
+
+    def mix(n, weights, v):
+        for h, (e, total) in enumerate(weights):
+            mixed = jnp.dot(e, v[:, h * 128:h * 128 + 128], preferred_element_type=f32)
+            a_buf[:, pl.ds((2 * n + h) * 128, 128)] = (mixed / total).astype(bf)
+
+    q, k, v = project(0)
+    held = None
     for n in range(8):
         ahead = project(n + 1) if n < 7 else None
-        mix(n, *held)
-        held = ahead
+        weights = weigh(q, k)
+        if held is not None:
+            mix(n - 1, *held)
+        held = (weights, v)
+        if ahead is not None:
+            q, k, v = ahead
+    mix(7, *held)
 
     for n in range(width // 512):
         cols = pl.ds(n * 512, 512)
         proj = jnp.dot(a_buf[...], to_ref[:, cols], preferred_element_type=f32).astype(bf)
         z_ref[:, cols] = (y_buf[:, cols].astype(f32) + proj.astype(f32)).astype(bf)
 
-    cp_h.wait_send()
-    each_m(lambda c: c.wait_send())
-    for u in range(6):
-        cp_own(u).wait_send()
-        for way in range(2):
-            cp_two(u, way).wait_send()
-            cp_one(u, way).wait_send()
-    every = range(6)
-    loop(9, lambda i: [cp_a(u, 1 + i // 3, 1 + i % 3).wait_send() for u in every])
-    loop(9, lambda i: [cp_b(u, 1 + i // 3, 1 + i % 3).wait_send() for u in every])
-    loop(3, lambda i: [cp_a0(u, 1 + i).wait_send() for u in every])
-    loop(3, lambda i: [cp_b0(u, 1 + i).wait_send() for u in every])
+    ring_left(late)
 
 
 def run_stage(o, ids, slots, gates, resid, scale, wq, wk, wv, wo):

time: 83.8 us -> 81.9 us (0.977)
  Pallas kernels: 82.9 us -> 81 us
    pallas_call x1, Pallas kernels: 82.9 us -> 81 us  [run_stage(): pl.pallas_call(stage_kernel, out_shape=pltpu.VMEM((tokens, width), bf), i...]
where the time goes in v3:
time: 81.9 us; the launch traced here: 81.8 us
  Pallas kernels  81 us (99%)
  local copies, waits for them, and re-layouts  0.82 us (1%)
    pallas_call x1, Pallas kernels, run_stage(): pl.pallas_call(stage_kernel, out_shape=pltpu.VMEM((tokens, width), bf), i...  81 us

profile of v3, /device:TPU:0, one launch (start us, length us, event | category | flops | bytes accessed | tf_op | source)
XLA Modules:
  0.0 81.8 jit_solution(8321241302457542933)
XLA Ops:
  0.0 81.0 %shard_map.100 = bf16[144,2048]{1,0:T(8,128)(2,1)S(1)} custom-call(bf16[4,4,4,24,2048]{4,3,2,1,0:T(8,128)(2,1)} %bitcast.15, s32[3,6,1,48]{3,2,1,0:T(1,128)} %bitcast.17, s32[3,6,1,48]{3,2,1,0:T(1,128)} %bitcast.18, f32[3,6,1,48]{3,2,1,0:T(1,128)} %bitcast.19, bf16[144,2048]{1,0:T(8,128)(2,1)} %bitcast.16, f32[1,2048]{1,0:T(1,128)} %scale_ref.1, ...), custom_call_target="tpu_custom_call" | custom-call | tf_op jit(solution)/shard_map/pallas_call | solution.py:324
  81.0 0.8 copy.12

commit v4 on v3

--- a/solution.py
+++ b/solution.py
@@ -150,7 +150,7 @@
                         at = (dc * n_seq + seq) * top_k + j
                         g = jnp.where(pos_t[0:LENGTH, at:at + 1] == lane, gate_t[0:LENGTH, at:at + 1], g)
                     for part in range(3):
-                        top = g.astype(bf)
+                        top = jnp.minimum(g, float(jnp.finfo(bf).max)).astype(bf)
                         g_buf[col, dc, pl.ds(part * tokens + seq * LENGTH, LENGTH), :] = top
                         g = g - top.astype(f32)
 

time: 81.9 us -> 81.9 us (level)
  no operation moved by 1% of the time
where the time goes in v4:
time: 81.9 us; the launch traced here: 81.8 us
  Pallas kernels  81 us (99%)
  local copies, waits for them, and re-layouts  0.82 us (1%)
    pallas_call x1, Pallas kernels, run_stage(): pl.pallas_call(stage_kernel, out_shape=pltpu.VMEM((tokens, width), bf), i...  81 us

profile of v4, /device:TPU:0, one launch (start us, length us, event | category | flops | bytes accessed | tf_op | source)
XLA Modules:
  0.0 81.8 jit_solution(2651878361025375077)
XLA Ops:
  0.0 81.0 %shard_map.100 = bf16[144,2048]{1,0:T(8,128)(2,1)S(1)} custom-call(bf16[4,4,4,24,2048]{4,3,2,1,0:T(8,128)(2,1)} %bitcast.15, s32[3,6,1,48]{3,2,1,0:T(1,128)} %bitcast.17, s32[3,6,1,48]{3,2,1,0:T(1,128)} %bitcast.18, f32[3,6,1,48]{3,2,1,0:T(1,128)} %bitcast.19, bf16[144,2048]{1,0:T(8,128)(2,1)} %bitcast.16, f32[1,2048]{1,0:T(1,128)} %scale_ref.1, ...), custom_call_target="tpu_custom_call" | custom-call | tf_op jit(solution)/shard_map/pallas_call | solution.py:324
  81.0 0.8 copy.12
